TPU v7x, 32 devices: a whole 2x2x4 slice. The times are simulated.
32 devices in a mesh: batch: 2 (over x), row: 4 (over z), col: 4 (over y, core).
Axes of the slice: x: 2, y: 2, z: 4, core: 2. Of those that a mesh axis runs over, the one named last changes fastest.
Arguments:
- tri_mat: bfloat16 [28672, 14336], P(('batch', 'row'), 'col'), parts along dimension 0
- rhs_mat: bfloat16 [28672, 4096], P(('batch', 'row'), 'col'), parts along dimension 0
Outputs:
- output: bfloat16 [28672, 4096], P(('batch', 'row'), 'col'), parts along dimension 0
There are 2 independent parts. A program takes and returns all parts, laid end to end along the dimension named above; each array names one.
All inputs are finite; a program needn't handle non-finite values.
Results may differ from a plain program's by a relative error of at most 0.001.
Values are sent between devices in bfloat16 or wider.
A program may use at most 1 GiB of HBM per device.

v0:
```python
import jax
import jax.numpy as jnp
from jax import lax
from jax.sharding import PartitionSpec as P

BLOCK_SIZE = 256


def solution(mesh):
    grid_rows = mesh.shape["row"]
    grid_cols = mesh.shape["col"]
    span = max(grid_rows, grid_cols)
    row_group = span // grid_rows * BLOCK_SIZE
    col_group = span // grid_cols * BLOCK_SIZE

    def local_trmm(tri_loc, rhs_loc):
        rows_loc = tri_loc.shape[0]
        cols_loc = rhs_loc.shape[1]
        num_steps = rows_loc // row_group
        finished = []
        running = None
        for step in range(num_steps):
            l_panel = tri_loc[step * row_group:, step * col_group:(step + 1) * col_group]
            b_panel = rhs_loc[step * row_group:(step + 1) * row_group]
            l_all = lax.all_gather(l_panel, "col")
            b_all = lax.all_gather(b_panel, "row")
            l_all = l_all.reshape(grid_cols, rows_loc - step * row_group, span // grid_cols, BLOCK_SIZE)
            b_all = b_all.reshape(grid_rows, span // grid_rows, BLOCK_SIZE, cols_loc).transpose(1, 0, 2, 3)
            b_all = b_all.reshape(span // grid_cols, grid_cols, BLOCK_SIZE, cols_loc)
            update = jnp.einsum("qrjc,jqcm->rm", l_all, b_all, preferred_element_type=jnp.float32)
            running = update if running is None else running + update
            finished.append(running[:row_group].astype(jnp.bfloat16))
            running = running[row_group:]
        return jnp.concatenate(finished, axis=0)

    part_spec = P(("batch", "row"), "col")
    return jax.shard_map(local_trmm, mesh=mesh, in_specs=(part_spec, part_spec), out_specs=part_spec, check_vma=False)
```

profile of v0, /device:TPU:0, one launch (start us, length us, event | category | flops | bytes accessed | tf_op | source)
XLA Modules:
  0.0 1132.7 jit_solution(10055162858449677226)
XLA Ops:
  6.5 6.0 fusion.16
  12.6 2.8 slice.175
  16.3 2.8 slice.179
  19.7 2.7 slice.183
  23.3 2.6 slice.187
  26.7 2.5 slice.191
  29.9 2.4 slice.195
  33.2 2.3 slice.199
  36.1 2.2 slice.203
  38.9 2.1 slice.207
  41.8 2.0 slice.211
  43.9 1.9 slice.215
  46.6 1.8 slice.219
  52.8 9.2 all-gather.26
  62.1 51.8 %all-gather.56.cloned.1.call-done = bf16[14336,256]{1,0:T(8,128)(2,1)} async-done(((bf16[3584,256]{1,0:T(8,128)(2,1)}), bf16[14336,256]{1,0:T(8,128)(2,1)}) %all-gather.56.cloned.1.call-update) | async-done | bytes 7340048 | tf_op jit(solution)/shard_map/all_gather | solution.py:25
  113.8 10.9 convolution_bitcast_fusion
  124.8 5.2 copy-done.9
  130.8 29.9 %all-gather.62.cloned.1.call-done = bf16[1024,1024]{1,0:T(8,128)(2,1)} async-done(((bf16[256,1024]{1,0:T(8,128)(2,1)}), bf16[1024,1024]{1,0:T(8,128)(2,1)}) %all-gather.62.cloned.1.call-update) | async-done | bytes 2097168 | tf_op jit(solution)/shard_map/all_gather | solution.py:26
  160.7 49.9 %all-gather.60.cloned.1.call-done = bf16[13312,256]{1,0:T(8,128)(2,1)} async-done(((bf16[3328,256]{1,0:T(8,128)(2,1)}), bf16[13312,256]{1,0:T(8,128)(2,1)}) %all-gather.60.cloned.1.call-update) | async-done | bytes 6815760 | tf_op jit(solution)/shard_map/all_gather | solution.py:25
  210.6 12.8 %slice_add_fusion = f32[3328,1024]{1,0:T(8,128)S(1)} fusion(f32[3584,1024]{1,0:T(8,128)} %copy-done.9, bf16[4,3328,256]{2,1,0:T(8,128)(2,1)} %bitcast.93, bf16[4,256,1024]{2,1,0:T(8,128)(2,1)} %bitcast.103), kind=kOutput, calls=%fused_computation | convolution fusion | flops 6982729728 | bytes 36175872 | tf_op jit(solution)/shard_map/qrjc,jqcm->rm/dot_general | solution.py:30
  223.5 4.9 copy-done.8
  229.2 28.1 %all-gather.66.cloned.1.call-done = bf16[1024,1024]{1,0:T(8,128)(2,1)} async-done(((bf16[256,1024]{1,0:T(8,128)(2,1)}), bf16[1024,1024]{1,0:T(8,128)(2,1)}) %all-gather.66.cloned.1.call-update) | async-done | bytes 2097168 | tf_op jit(solution)/shard_map/all_gather | solution.py:26
  257.3 46.9 %all-gather.64.cloned.1.call-done = bf16[12288,256]{1,0:T(8,128)(2,1)} async-done(((bf16[3072,256]{1,0:T(8,128)(2,1)}), bf16[12288,256]{1,0:T(8,128)(2,1)}) %all-gather.64.cloned.1.call-update) | async-done | bytes 6291472 | tf_op jit(solution)/shard_map/all_gather | solution.py:25
  304.2 11.7 %slice_add_fusion.1 = f32[3072,1024]{1,0:T(8,128)S(1)} fusion(f32[3328,1024]{1,0:T(8,128)} %copy-done.8, bf16[4,3072,256]{2,1,0:T(8,128)(2,1)} %bitcast.94, bf16[4,256,1024]{2,1,0:T(8,128)(2,1)} %bitcast.104), kind=kOutput, calls=%fused_computation.1 | convolution fusion | flops 6445596672 | bytes 33554432 | tf_op jit(solution)/shard_map/qrjc,jqcm->rm/dot_general | solution.py:30
  315.9 4.6 copy-done.7
  321.4 29.7 %all-gather.70.cloned.1.call-done = bf16[1024,1024]{1,0:T(8,128)(2,1)} async-done(((bf16[256,1024]{1,0:T(8,128)(2,1)}), bf16[1024,1024]{1,0:T(8,128)(2,1)}) %all-gather.70.cloned.1.call-update) | async-done | bytes 2097168 | tf_op jit(solution)/shard_map/all_gather | solution.py:26
  351.1 44.0 %all-gather.68.cloned.1.call-done = bf16[11264,256]{1,0:T(8,128)(2,1)} async-done(((bf16[2816,256]{1,0:T(8,128)(2,1)}), bf16[11264,256]{1,0:T(8,128)(2,1)}) %all-gather.68.cloned.1.call-update) | async-done | bytes 5767184 | tf_op jit(solution)/shard_map/all_gather | solution.py:25
  395.0 15.2 %slice_add_fusion.2 = f32[2816,1024]{1,0:T(8,128)S(1)} fusion(f32[3072,1024]{1,0:T(8,128)} %copy-done.7, bf16[4,2816,256]{2,1,0:T(8,128)(2,1)} %bitcast.95, bf16[4,256,1024]{2,1,0:T(8,128)(2,1)} %bitcast.105), kind=kOutput, calls=%fused_computation.2 | convolution fusion | flops 5908463616 | bytes 30932992 | tf_op jit(solution)/shard_map/qrjc,jqcm->rm/dot_general | solution.py:30
  410.3 4.2 copy-done.6
  415.3 26.6 %all-gather.74.cloned.1.call-done = bf16[1024,1024]{1,0:T(8,128)(2,1)} async-done(((bf16[256,1024]{1,0:T(8,128)(2,1)}), bf16[1024,1024]{1,0:T(8,128)(2,1)}) %all-gather.74.cloned.1.call-update) | async-done | bytes 2097168 | tf_op jit(solution)/shard_map/all_gather | solution.py:26
  441.9 40.8 %all-gather.72.cloned.1.call-done = bf16[10240,256]{1,0:T(8,128)(2,1)} async-done(((bf16[2560,256]{1,0:T(8,128)(2,1)}), bf16[10240,256]{1,0:T(8,128)(2,1)}) %all-gather.72.cloned.1.call-update) | async-done | bytes 5242896 | tf_op jit(solution)/shard_map/all_gather | solution.py:25
  482.7 13.5 %slice_add_fusion.3 = f32[2560,1024]{1,0:T(8,128)S(1)} fusion(f32[2816,1024]{1,0:T(8,128)} %copy-done.6, bf16[4,2560,256]{2,1,0:T(8,128)(2,1)} %bitcast.96, bf16[4,256,1024]{2,1,0:T(8,128)(2,1)} %bitcast.106), kind=kOutput, calls=%fused_computation.3 | convolution fusion | flops 5371330560 | bytes 28311552 | tf_op jit(solution)/shard_map/qrjc,jqcm->rm/dot_general | solution.py:30
  496.2 4.0 copy-done.5
  501.1 28.5 %all-gather.78.cloned.1.call-done = bf16[1024,1024]{1,0:T(8,128)(2,1)} async-done(((bf16[256,1024]{1,0:T(8,128)(2,1)}), bf16[1024,1024]{1,0:T(8,128)(2,1)}) %all-gather.78.cloned.1.call-update) | async-done | bytes 2097168 | tf_op jit(solution)/shard_map/all_gather | solution.py:26
  529.6 37.8 %all-gather.76.cloned.1.call-done = bf16[9216,256]{1,0:T(8,128)(2,1)} async-done(((bf16[2304,256]{1,0:T(8,128)(2,1)}), bf16[9216,256]{1,0:T(8,128)(2,1)}) %all-gather.76.cloned.1.call-update) | async-done | bytes 4718608 | tf_op jit(solution)/shard_map/all_gather | solution.py:25
  567.4 12.7 %slice_add_fusion.4 = f32[2304,1024]{1,0:T(8,128)S(1)} fusion(f32[2560,1024]{1,0:T(8,128)} %copy-done.5, bf16[4,2304,256]{2,1,0:T(8,128)(2,1)} %bitcast.97, bf16[4,256,1024]{2,1,0:T(8,128)(2,1)} %bitcast.107), kind=kOutput, calls=%fused_computation.4 | convolution fusion | flops 4834197504 | bytes 25690112 | tf_op jit(solution)/shard_map/qrjc,jqcm->rm/dot_general | solution.py:30
  580.1 3.7 copy-done.4
  584.6 29.6 %all-gather.82.cloned.1.call-done = bf16[1024,1024]{1,0:T(8,128)(2,1)} async-done(((bf16[256,1024]{1,0:T(8,128)(2,1)}), bf16[1024,1024]{1,0:T(8,128)(2,1)}) %all-gather.82.cloned.1.call-update) | async-done | bytes 2097168 | tf_op jit(solution)/shard_map/all_gather | solution.py:26
  614.2 34.8 %all-gather.80.cloned.1.call-done = bf16[8192,256]{1,0:T(8,128)(2,1)} async-done(((bf16[2048,256]{1,0:T(8,128)(2,1)}), bf16[8192,256]{1,0:T(8,128)(2,1)}) %all-gather.80.cloned.1.call-update) | async-done | bytes 4194320 | tf_op jit(solution)/shard_map/all_gather | solution.py:25
  649.0 10.3 slice_add_fusion.5
  659.3 3.3 copy-done.3
  663.5 32.2 %all-gather.86.cloned.1.call-done = bf16[1024,1024]{1,0:T(8,128)(2,1)} async-done(((bf16[256,1024]{1,0:T(8,128)(2,1)}), bf16[1024,1024]{1,0:T(8,128)(2,1)}) %all-gather.86.cloned.1.call-update) | async-done | bytes 2097168 | tf_op jit(solution)/shard_map/all_gather | solution.py:26
  695.7 31.7 %all-gather.84.cloned.1.call-done = bf16[7168,256]{1,0:T(8,128)(2,1)} async-done(((bf16[1792,256]{1,0:T(8,128)(2,1)}), bf16[7168,256]{1,0:T(8,128)(2,1)}) %all-gather.84.cloned.1.call-update) | async-done | bytes 3670032 | tf_op jit(solution)/shard_map/all_gather | solution.py:25
  727.4 11.7 %slice_add_fusion.6 = f32[1792,1024]{1,0:T(8,128)} fusion(f32[2048,1024]{1,0:T(8,128)} %copy-done.3, bf16[4,1792,256]{2,1,0:T(8,128)(2,1)} %bitcast.99, bf16[4,256,1024]{2,1,0:T(8,128)(2,1)} %bitcast.109), kind=kOutput, calls=%fused_computation.7 | convolution fusion | flops 3759931392 | bytes 20447232 | tf_op jit(solution)/shard_map/qrjc,jqcm->rm/dot_general | solution.py:30
  739.1 35.0 %all-gather.90.cloned.1.call-done = bf16[1024,1024]{1,0:T(8,128)(2,1)} async-done(((bf16[256,1024]{1,0:T(8,128)(2,1)}), bf16[1024,1024]{1,0:T(8,128)(2,1)}) %all-gather.90.cloned.1.call-update) | async-done | bytes 2097168 | tf_op jit(solution)/shard_map/all_gather | solution.py:26
  774.1 28.7 %all-gather.88.cloned.1.call-done = bf16[6144,256]{1,0:T(8,128)(2,1)} async-done(((bf16[1536,256]{1,0:T(8,128)(2,1)}), bf16[6144,256]{1,0:T(8,128)(2,1)}) %all-gather.88.cloned.1.call-update) | async-done | bytes 3145744 | tf_op jit(solution)/shard_map/all_gather | solution.py:25
  802.9 10.4 slice_add_fusion.7
  813.3 36.4 %all-gather.94.cloned.1.call-done = bf16[1024,1024]{1,0:T(8,128)(2,1)} async-done(((bf16[256,1024]{1,0:T(8,128)(2,1)}), bf16[1024,1024]{1,0:T(8,128)(2,1)}) %all-gather.94.cloned.1.call-update) | async-done | bytes 2097168 | tf_op jit(solution)/shard_map/all_gather | solution.py:26
  849.7 25.7 %all-gather.92.cloned.1.call-done = bf16[5120,256]{1,0:T(8,128)(2,1)} async-done(((bf16[1280,256]{1,0:T(8,128)(2,1)}), bf16[5120,256]{1,0:T(8,128)(2,1)}) %all-gather.92.cloned.1.call-update) | async-done | bytes 2621456 | tf_op jit(solution)/shard_map/all_gather | solution.py:25
  875.4 7.1 slice_add_fusion.8
  882.5 2.9 fusion.10
  885.4 2.1 fusion.11
  888.3 11.0 all-gather.96.cloned.1.call-done
  899.3 46.9 %all-gather.98.cloned.1.call-done = bf16[1024,1024]{1,0:T(8,128)(2,1)} async-done(((bf16[256,1024]{1,0:T(8,128)(2,1)}), bf16[1024,1024]{1,0:T(8,128)(2,1)}) %all-gather.98.cloned.1.call-update) | async-done | bytes 2097168 | tf_op jit(solution)/shard_map/all_gather | solution.py:26
  946.2 5.8 slice_add_fusion.9
  952.0 2.0 copy-done.1
  954.9 11.3 %all-gather.100.cloned.1.call-done = bf16[3072,256]{1,0:T(8,128)(2,1)} async-done(((bf16[768,256]{1,0:T(8,128)(2,1)}), bf16[3072,256]{1,0:T(8,128)(2,1)}) %all-gather.100.cloned.1.call-update) | async-done | bytes 1572880 | tf_op jit(solution)/shard_map/all_gather | solution.py:25
  966.2 46.7 %all-gather.102.cloned.1.call-done = bf16[1024,1024]{1,0:T(8,128)(2,1)} async-done(((bf16[256,1024]{1,0:T(8,128)(2,1)}), bf16[1024,1024]{1,0:T(8,128)(2,1)}) %all-gather.102.cloned.1.call-update) | async-done | bytes 2097168 | tf_op jit(solution)/shard_map/all_gather | solution.py:26
  1012.9 4.8 slice_add_fusion.10
  1020.2 9.8 all-gather.104.cloned.1.call-done
  1030.0 46.7 %all-gather.106.cloned.1.call-done = bf16[1024,1024]{1,0:T(8,128)(2,1)} async-done(((bf16[256,1024]{1,0:T(8,128)(2,1)}), bf16[1024,1024]{1,0:T(8,128)(2,1)}) %all-gather.106.cloned.1.call-update) | async-done | bytes 2097168 | tf_op jit(solution)/shard_map/all_gather | solution.py:26
  1076.8 3.8 slice_add_fusion.11
  1081.4 41.1 %all-gather.108.cloned.1.call-done = bf16[1024,1024]{1,0:T(8,128)(2,1)} async-done(((bf16[256,1024]{1,0:T(8,128)(2,1)}), bf16[1024,1024]{1,0:T(8,128)(2,1)}) %all-gather.108.cloned.1.call-update) | async-done | bytes 2097168 | tf_op jit(solution)/shard_map/all_gather | solution.py:26
  1122.5 3.1 fusion.2
  (80 shorter events, 23.1 us)
Async XLA Ops:
  6.5 55.5 %all-gather.58.cloned.1.call-start = ((), (), s32[]{:S(2)}) async-start(), calls=%async_computation.1 | async-start | bytes 2621440 | tf_op jit(solution)/shard_map/all_gather | solution.py:26
  12.6 101.2 %all-gather.56.cloned.1.call-start = ((), (), s32[]{:S(2)}) async-start(), calls=%async_computation | async-start | bytes 9175040 | tf_op jit(solution)/shard_map/all_gather | solution.py:25
  15.5 145.2 %all-gather.62.cloned.1.call-start = ((), (), s32[]{:S(2)}) async-start(), calls=%async_computation.3 | async-start | bytes 2621440 | tf_op jit(solution)/shard_map/all_gather | solution.py:26
  16.3 194.4 %all-gather.60.cloned.1.call-start = ((), (), s32[]{:S(2)}) async-start(), calls=%async_computation.2 | async-start | bytes 8519680 | tf_op jit(solution)/shard_map/all_gather | solution.py:25
  19.1 238.2 %all-gather.66.cloned.1.call-start = ((), (), s32[]{:S(2)}) async-start(), calls=%async_computation.5 | async-start | bytes 2621440 | tf_op jit(solution)/shard_map/all_gather | solution.py:26
  19.7 284.5 %all-gather.64.cloned.1.call-start = ((), (), s32[]{:S(2)}) async-start(), calls=%async_computation.4 | async-start | bytes 7864320 | tf_op jit(solution)/shard_map/all_gather | solution.py:25
  22.5 328.6 %all-gather.70.cloned.1.call-start = ((), (), s32[]{:S(2)}) async-start(), calls=%async_computation.7 | async-start | bytes 2621440 | tf_op jit(solution)/shard_map/all_gather | solution.py:26
  23.2 371.8 %all-gather.68.cloned.1.call-start = ((), (), s32[]{:S(2)}) async-start(), calls=%async_computation.6 | async-start | bytes 7208960 | tf_op jit(solution)/shard_map/all_gather | solution.py:25
  25.9 416.0 %all-gather.74.cloned.1.call-start = ((), (), s32[]{:S(2)}) async-start(), calls=%async_computation.9 | async-start | bytes 2621440 | tf_op jit(solution)/shard_map/all_gather | solution.py:26
  26.6 456.1 %all-gather.72.cloned.1.call-start = ((), (), s32[]{:S(2)}) async-start(), calls=%async_computation.8 | async-start | bytes 6553600 | tf_op jit(solution)/shard_map/all_gather | solution.py:25
  29.1 500.5 %all-gather.78.cloned.1.call-start = ((), (), s32[]{:S(2)}) async-start(), calls=%async_computation.11 | async-start | bytes 2621440 | tf_op jit(solution)/shard_map/all_gather | solution.py:26
  29.9 537.5 %all-gather.76.cloned.1.call-start = ((), (), s32[]{:S(2)}) async-start(), calls=%async_computation.10 | async-start | bytes 5898240 | tf_op jit(solution)/shard_map/all_gather | solution.py:25
  32.4 581.9 %all-gather.82.cloned.1.call-start = ((), (), s32[]{:S(2)}) async-start(), calls=%async_computation.13 | async-start | bytes 2621440 | tf_op jit(solution)/shard_map/all_gather | solution.py:26
  33.1 615.9 %all-gather.80.cloned.1.call-start = ((), (), s32[]{:S(2)}) async-start(), calls=%async_computation.12 | async-start | bytes 5242880 | tf_op jit(solution)/shard_map/all_gather | solution.py:25
  35.5 660.2 %all-gather.86.cloned.1.call-start = ((), (), s32[]{:S(2)}) async-start(), calls=%async_computation.15 | async-start | bytes 2621440 | tf_op jit(solution)/shard_map/all_gather | solution.py:26
  36.0 691.4 %all-gather.84.cloned.1.call-start = ((), (), s32[]{:S(2)}) async-start(), calls=%async_computation.14 | async-start | bytes 4587520 | tf_op jit(solution)/shard_map/all_gather | solution.py:25
  38.3 735.9 %all-gather.90.cloned.1.call-start = ((), (), s32[]{:S(2)}) async-start(), calls=%async_computation.17 | async-start | bytes 2621440 | tf_op jit(solution)/shard_map/all_gather | solution.py:26
  38.9 764.0 %all-gather.88.cloned.1.call-start = ((), (), s32[]{:S(2)}) async-start(), calls=%async_computation.16 | async-start | bytes 3932160 | tf_op jit(solution)/shard_map/all_gather | solution.py:25
  41.0 808.7 %all-gather.94.cloned.1.call-start = ((), (), s32[]{:S(2)}) async-start(), calls=%async_computation.19 | async-start | bytes 2621440 | tf_op jit(solution)/shard_map/all_gather | solution.py:26
  41.8 833.6 %all-gather.92.cloned.1.call-start = ((), (), s32[]{:S(2)}) async-start(), calls=%async_computation.18 | async-start | bytes 3276800 | tf_op jit(solution)/shard_map/all_gather | solution.py:25
  43.8 855.5 %all-gather.96.cloned.1.call-start = ((), (), s32[]{:S(2)}) async-start(), calls=%async_computation.20 | async-start | bytes 2621440 | tf_op jit(solution)/shard_map/all_gather | solution.py:25
  45.8 900.4 %all-gather.98.cloned.1.call-start = ((), (), s32[]{:S(2)}) async-start(), calls=%async_computation.21 | async-start | bytes 2621440 | tf_op jit(solution)/shard_map/all_gather | solution.py:26
  46.5 919.7 %all-gather.100.cloned.1.call-start = ((), (), s32[]{:S(2)}) async-start(), calls=%async_computation.22 | async-start | bytes 1966080 | tf_op jit(solution)/shard_map/all_gather | solution.py:25
  48.4 964.5 %all-gather.102.cloned.1.call-start = ((), (), s32[]{:S(2)}) async-start(), calls=%async_computation.23 | async-start | bytes 2621440 | tf_op jit(solution)/shard_map/all_gather | solution.py:26
  49.0 981.1 %all-gather.104.cloned.1.call-start = ((), (), s32[]{:S(2)}) async-start(), calls=%async_computation.24 | async-start | bytes 1310720 | tf_op jit(solution)/shard_map/all_gather | solution.py:25
  50.7 1026.0 %all-gather.106.cloned.1.call-start = ((), (), s32[]{:S(2)}) async-start(), calls=%async_computation.25 | async-start | bytes 2621440 | tf_op jit(solution)/shard_map/all_gather | solution.py:26
  51.3 1071.2 %all-gather.108.cloned.1.call-start = ((), (), s32[]{:S(2)}) async-start(), calls=%async_computation.26 | async-start | bytes 2621440 | tf_op jit(solution)/shard_map/all_gather | solution.py:26
  124.8 5.2 copy-start.9
  223.5 4.9 copy-start.8
  315.9 4.6 copy-start.7
  410.3 4.2 copy-start.6
  496.2 4.0 copy-start.5
  580.1 3.7 copy-start.4
  659.3 3.4 copy-start.3
  882.5 5.0 copy-start.2
  952.0 2.0 copy-start.1
  1017.7 1.6 copy-start
Sparse Core Ops, SparseCore 0:
  12.7 48.0 all-gather.57
  62.3 51.4 all-gather.55
  115.4 45.2 all-gather.61
  162.1 48.4 all-gather.59
  212.0 45.2 all-gather.65
  258.7 45.4 all-gather.63
  305.8 45.2 all-gather.69
  352.6 42.3 all-gather.67
  396.6 45.2 all-gather.73
  443.3 39.3 all-gather.71
  484.3 45.2 all-gather.77
  531.0 36.3 all-gather.75
  568.9 45.2 all-gather.81
  615.6 33.2 all-gather.79
  650.4 45.2 all-gather.85
  697.1 30.2 all-gather.83
  728.9 45.2 all-gather.89
  775.6 27.2 all-gather.87
  804.4 45.2 all-gather.93
  851.1 24.2 all-gather.91
  877.0 22.3 all-gather.95
  900.9 45.2 all-gather.97
  947.7 18.4 all-gather.99
  967.6 45.2 all-gather.101
  1014.5 15.5 all-gather.103
  1031.5 45.2 all-gather.105
  1078.2 44.2 all-gather.107
where the time goes:
time: 1140 us; the launch traced here: 1130 us
  waiting for transfers between devices  890 us (78%)
  matrix products  134 us (12%)
  local copies, waits for them, and re-layouts  84.6 us (7%)
  between operations  14.3 us (1%)
    all_gather x14, waiting for transfers between devices, local_trmm(): b_all = lax.all_gather(b_panel, 'row')  457 us
    all_gather x13, waiting for transfers between devices, local_trmm(): l_all = lax.all_gather(l_panel, 'col')  424 us
    dot_general x14, matrix products, local_trmm(): jnp.einsum('qrjc,jqcm->rm', l_all, b_all, preferred_element_type=jnp.floa...  134 us
    unnamed x33, local copies, waits for them, and re-layouts  48 us
    slice x14, local copies, waits for them, and re-layouts, local_trmm(): tri_loc[step * row_group:, step * col_group:(step + 1) * col_group]  30.5 us
  transfers between devices with their start and end apart: 27, of which 26 were waited for; matrix products, arithmetic and copies ran while one was open for 16% of the time, Pallas kernels for 0%

commit v1 on v0

v1 whole, which is shorter than its diff:
```python
import functools

import jax
import jax.numpy as jnp
from jax import lax
from jax.experimental import pallas as pl
from jax.experimental.pallas import tpu as pltpu
from jax.sharding import PartitionSpec as P

BLOCK_SIZE = 256
NEAR_STEPS = 6
LAG = 3
AHEAD = 4
SLOTS = 4
MESH = pl.DeviceIdType.MESH


def flip(v, t):
    if t == 0:
        return v
    if t == 1:
        return v + 1 - 2 * lax.rem(v, 2)
    if t == 2:
        return lax.rem(v + 2, 4)
    return 3 - v


def xor(a, b):
    return lax.rem(a + b, 2) + 2 * lax.rem(a // 2 + b // 2, 2)


def kernel(bs, nb, near, tri, rhs, out, l_got, l_end, b_got, acc, part, l_tile, b_tile, o_tile, sems, l_sem, b_sem, o_sem):
    (ys, yr, ds, dr, fs, fr, b1s, b1r, l0s, l0r, l2s, l2r, e0s, e0r, e2s, e2r,
     os_, or_, ws, wr, ms, mr, us, ur, vs, vr, ps, pr) = sems
    g, z, c = lax.axis_index("batch"), lax.axis_index("row"), lax.axis_index("col")
    is_end = lax.rem(z, 3) == 0
    ze = flip(z, 1)
    zo = flip(z, 3)
    sib, across = flip(c, 1), flip(c, 2)

    def rows(s):
        return pl.ds(pl.multiple_of(s * bs, bs), bs)

    def panel(ref, s, n=None):
        at = (pl.ds(s * bs, (nb - s) * bs), pl.ds(s * bs, bs))
        return ref.at[at] if n is None else ref.at[(n,) + at]

    def send(src, dst, ss, rs, dev):
        return pltpu.make_async_remote_copy(src_ref=src, dst_ref=dst, send_sem=ss, recv_sem=rs, device_id=dev, device_id_type=MESH)

    def y_copy(s):
        return send(panel(tri, s), panel(l_got, s, 1), ys.at[s], yr.at[s], (g, z, across))

    def d_copy(s):
        return send(panel(tri, s), panel(l_got, s, 0), ds.at[s], dr.at[s], (g, z, sib))

    def f_copy(s):
        return send(panel(l_got, s, 1), panel(l_got, s, 2), fs.at[s], fr.at[s], (g, z, sib))

    def l0_copy(s):
        return send(panel(tri, s), panel(l_end, s, 0), l0s.at[s - near], l0r.at[s - near], (g, ze, c))

    def l2_copy(s):
        return send(panel(l_got, s, 1), panel(l_end, s, 2), l2s.at[s - near], l2r.at[s - near], (g, ze, c))

    def e0_copy(s):
        return send(panel(l_end, s, 0), panel(l_end, s, 1), e0s.at[s - near], e0r.at[s - near], (g, z, sib))

    def e2_copy(s):
        return send(panel(l_end, s, 2), panel(l_end, s, 3), e2s.at[s - near], e2r.at[s - near], (g, z, sib))

    def b_copy(owner, n, ss, rs, dev):
        return send(rhs.at[rows(n)], b_got.at[owner, rows(n)], ss.at[n], rs.at[n], dev)

    def b_forward(owner, n, ss, rs, dev):
        return send(b_got.at[owner, rows(n)], b_got.at[owner, rows(n)], ss.at[n], rs.at[n], dev)

    def b1_copy(n):
        return b_copy(z, n, b1s, b1r, (g, ze, c))

    def o_copy(n):
        return b_copy(z, n, os_, or_, (g, zo, c))

    def w_copy(n):
        return b_forward(ze, n, ws, wr, (g, zo, c))

    def m_copy(n):
        return b_copy(z, n, ms, mr, (g, ze, c))

    def u_copy(n):
        return b_forward(zo, n, us, ur, (g, ze, c))

    def v_copy(n):
        return b_forward(flip(zo, 1), n, vs, vr, (g, ze, c))

    def p_copy(j):
        at = pl.ds(pl.multiple_of((j - near) * bs, bs), bs)
        return send(part.at[at], part.at[at], ps.at[j - near], pr.at[j - near], (g, ze, c))

    def at_step(s, lo, hi, fn):
        for i in range(lo, hi):
            @pl.when(s == i)
            def _():
                fn(i)

    def pass_on(s):
        y_copy(s).wait_recv()
        f_copy(s).start()

    def load_b(slots):
        for i, owner in slots:
            to = b_tile.at[pl.ds(i * bs, bs)]

            @pl.when(owner == z)
            def _():
                pltpu.make_async_copy(rhs.at[rows(load_b.step)], to, b_sem.at[i]).start()

            @pl.when(owner != z)
            def _():
                pltpu.make_async_copy(b_got.at[owner, rows(load_b.step)], to, b_sem.at[i]).start()
        for i, owner in slots:
            pltpu.make_async_copy(rhs.at[rows(0)], b_tile.at[pl.ds(i * bs, bs)], b_sem.at[i]).wait()

    def tiles(s, start_tile, depth, target, base):
        def start(j):
            start_tile(j, lax.rem(j - s, SLOTS))

        def wait(slot):
            for i in range(depth):
                to = l_tile.at[slot, :, pl.ds(i * bs, bs)]
                pltpu.make_async_copy(tri.at[pl.ds(0, bs), pl.ds(0, bs)], to, l_sem.at[slot, i]).wait()

        for d in range(SLOTS - 1):
            @pl.when(s + d < nb)
            def _():
                start(s + d)

        @pl.loop(s, nb)
        def _(j):
            @pl.when(j + SLOTS - 1 < nb)
            def _():
                start(j + SLOTS - 1)

            slot = lax.rem(j - s, SLOTS)
            wait(slot)
            at = pl.ds(pl.multiple_of((j - base) * bs, bs), bs)
            target[at, :] += jnp.dot(
                l_tile[slot, :, : depth * bs], b_tile[: depth * bs, :], preferred_element_type=jnp.float32
            )

    def l_copy(ref, j, s, slot, i):
        to = l_tile.at[slot, :, pl.ds(i * bs, bs)]
        return pltpu.make_async_copy(ref.at[rows(j), rows(s)], to, l_sem.at[slot, i])

    def own_step(s):
        load_b.step = s
        load_b([(r, flip(c, r)) for r in range(4)])

        def start_tile(j, slot):
            l_copy(tri, j, s, slot, 0).start()
            for r in range(1, 4):
                l_copy(l_got.at[r - 1], j, s, slot, r).start()

        tiles(s, start_tile, 4, acc, 0)

    def diag_step(s):
        load_b.step = s
        load_b([(0, z)])
        r = xor(c, z)

        def start_tile(j, slot):
            @pl.when(r == 0)
            def _():
                l_copy(tri, j, s, slot, 0).start()

            for k in range(1, 4):
                @pl.when(r == k)
                def _():
                    l_copy(l_got.at[k - 1], j, s, slot, 0).start()

        tiles(s, start_tile, 1, acc, 0)

    def end_step(s):
        load_b.step = s
        load_b([(t - 1, flip(ze, t)) for t in range(1, 4)])
        r0 = xor(c, ze)

        def start_tile(j, slot):
            for t in range(1, 4):
                l_copy(l_end.at[flip(r0, t)], j, s, slot, t - 1).start()

        tiles(s, start_tile, 3, part, near)

    def finish(j, extra):
        at = rows(j)
        total = acc[at, :]
        if extra:
            total = total + part[pl.ds(pl.multiple_of((j - near) * bs, bs), bs), :]
        o_tile[...] = total.astype(o_tile.dtype)
        copy = pltpu.make_async_copy(o_tile, out.at[at], o_sem)
        copy.start()
        copy.wait()

    has0, has2 = c != ze, across != ze
    gives0, gives2 = c != z, across != z

    @pl.when(is_end)
    def _():
        for s in list(range(near, nb)) + list(range(near)):
            y_copy(s).start()
        for s in range(nb):
            d_copy(s).start()
        sent = 0
        for j in range(near, nb):
            upto = min(4 + 2 * (j - near), j + 2) if j < nb - 1 else nb - 2
            for n in range(sent, upto):
                b1_copy(n).start()
            sent = max(sent, upto)
            pass_on(j)

            @pl.when(gives0)
            def _():
                l0_copy(j).start()

            @pl.when(gives2)
            def _():
                l2_copy(j).start()

        for n in range(sent, nb):
            b1_copy(n).start()

        acc[...] = jnp.zeros_like(acc)

        @pl.loop(near, nb)
        def _(s):
            def ready(i):
                d_copy(i).wait_recv()
                f_copy(i).wait_recv()

            at_step(s, near, nb, ready)
            diag_step(s)

        @pl.loop(0, near)
        def _(s):
            def ready(i):
                pass_on(i)
                d_copy(i).wait_recv()
                f_copy(i).wait_recv()

            at_step(s, 0, near, ready)
            for copy in (m_copy, u_copy, v_copy):
                copy(s).wait_recv()
            own_step(s)
            finish(s, False)

        @pl.loop(near, nb)
        def _(j):
            p_copy(j).wait_recv()
            finish(j, True)

        for s in range(nb):
            y_copy(s).wait_send()
            d_copy(s).wait_send()
            f_copy(s).wait_send()
            b1_copy(s).wait_send()
        for s in range(near, nb):
            @pl.when(gives0)
            def _():
                l0_copy(s).wait_send()

            @pl.when(gives2)
            def _():
                l2_copy(s).wait_send()

    @pl.when(jnp.logical_not(is_end))
    def _():
        for n in range(AHEAD):
            o_copy(n).start()
        for n in range(near):
            m_copy(n).start()
        for s in range(nb):
            y_copy(s).start()
        for s in range(nb):
            d_copy(s).start()
        acc[...] = jnp.zeros_like(acc)
        part[...] = jnp.zeros_like(part)

        @pl.loop(0, nb + LAG)
        def _(n):
            @pl.when(n < nb)
            def _():
                b1_copy(n).wait_recv()
                w_copy(n).start()

                @pl.when(n + AHEAD < nb)
                def _():
                    o_copy(n + AHEAD).start()

                o_copy(n).wait_recv()
                w_copy(n).wait_recv()

                @pl.when(n < near)
                def _():
                    u_copy(n).start()
                    v_copy(n).start()

                @pl.when(n >= near)
                def _():
                    def relay(i):
                        @pl.when(has0)
                        def _():
                            l0_copy(i).wait_recv()
                            e0_copy(i).start()

                        @pl.when(has2)
                        def _():
                            l2_copy(i).wait_recv()
                            e2_copy(i).start()

                        @pl.when(sib != ze)
                        def _():
                            e0_copy(i).wait_recv()

                        @pl.when(3 - c != ze)
                        def _():
                            e2_copy(i).wait_recv()

                    at_step(n, near, nb, relay)
                    end_step(n)
                    p_copy(n).start()

            @pl.when(n >= LAG)
            def _():
                s = n - LAG

                def ready(i):
                    pass_on(i)
                    d_copy(i).wait_recv()
                    f_copy(i).wait_recv()

                at_step(s, 0, nb, ready)
                own_step(s)
                finish(s, False)

        for s in range(nb):
            y_copy(s).wait_send()
            d_copy(s).wait_send()
            f_copy(s).wait_send()
            o_copy(s).wait_send()
            w_copy(s).wait_send()
        for s in range(near):
            m_copy(s).wait_send()
            u_copy(s).wait_send()
            v_copy(s).wait_send()
        for s in range(near, nb):
            p_copy(s).wait_send()

            @pl.when(has0)
            def _():
                e0_copy(s).wait_send()

            @pl.when(has2)
            def _():
                e2_copy(s).wait_send()


def local_trmm(tri, rhs, bs=BLOCK_SIZE, near=NEAR_STEPS):
    size, cols = rhs.shape
    nb = size // bs
    far = nb - near
    any_spec = pl.BlockSpec(memory_space=pl.ANY)
    counts = [nb] * 8 + [far] * 8 + [nb] * 4 + [near] * 6 + [far] * 2
    return pl.pallas_call(
        functools.partial(kernel, bs, nb, near),
        out_shape=[
            jax.ShapeDtypeStruct((size, cols), jnp.bfloat16),
            jax.ShapeDtypeStruct((3, size, size), jnp.bfloat16),
            jax.ShapeDtypeStruct((4, size, size), jnp.bfloat16),
            jax.ShapeDtypeStruct((4, size, cols), jnp.bfloat16),
        ],
        in_specs=[any_spec] * 2,
        out_specs=[any_spec] * 4,
        scratch_shapes=[
            pltpu.VMEM((size, cols), jnp.float32),
            pltpu.VMEM((far * bs, cols), jnp.float32),
            pltpu.VMEM((SLOTS, bs, 4 * bs), jnp.bfloat16),
            pltpu.VMEM((4 * bs, cols), jnp.bfloat16),
            pltpu.VMEM((bs, cols), jnp.bfloat16),
            tuple(pltpu.SemaphoreType.DMA((n,)) for n in counts),
            pltpu.SemaphoreType.DMA((SLOTS, 4)),
            pltpu.SemaphoreType.DMA((4,)),
            pltpu.SemaphoreType.DMA,
        ],
        compiler_params=pltpu.CompilerParams(has_side_effects=True, vmem_limit_bytes=56 * 2**20),
    )(tri, rhs)[0]


def solution(mesh):
    part_spec = P(("batch", "row"), "col")
    return jax.shard_map(local_trmm, mesh=mesh, in_specs=(part_spec, part_spec), out_specs=part_spec, check_vma=False)
```

time: 1140 us -> 489 us (0.43)
  waiting for transfers between devices: 890 us -> 0 us
  Pallas kernels: 0 us -> 480 us
  matrix products: 134 us -> 0 us
  local copies, waits for them, and re-layouts: 84.6 us -> 6.98 us
  between operations: 14.3 us -> 0.01 us
    all_gather x27 -> x0, waiting for transfers between devices: 882 us -> none  [the longest x14 457 us: local_trmm(): b_all = lax.all_gather(b_panel, 'row')]
    pallas_call x0 -> x1, Pallas kernels: none -> 480 us  [local_trmm(): pl.pallas_call(functools.partial(kernel, bs, nb, near), out_shape=[jax.Sh...]
    dot_general x14 -> x0, matrix products: 134 us -> none  [local_trmm(): jnp.einsum('qrjc,jqcm->rm', l_all, b_all, preferred_element_type=jnp.floa...]
    unnamed x33 -> x1, local copies, waits for them, and re-layouts: 48 us -> 6.98 us
    slice x15 -> x0, local copies, waits for them, and re-layouts: 36.6 us -> none  [the longest x14 30.5 us: local_trmm(): tri_loc[step * row_group:, step * col_group:(step + 1) * col_group]]
  transfers between devices with their start and end apart: 27 -> 0, of which waited for: 26 -> 0; matrix products, arithmetic and copies ran while one was open for 16% -> 0% of each run, Pallas kernels for 0% -> 0%
where the time goes in v1:
time: 489 us; the launch traced here: 487 us
  Pallas kernels  480 us (98%)
  local copies, waits for them, and re-layouts  6.98 us (1%)
    pallas_call x1, Pallas kernels, local_trmm(): pl.pallas_call(functools.partial(kernel, bs, nb, near), out_shape=[jax.Sh...  480 us

profile of v1, /device:TPU:0, one launch (start us, length us, event | category | flops | bytes accessed | tf_op | source)
XLA Modules:
  0.0 487.4 jit_solution(10199310341768716354)
XLA Ops:
  0.0 480.4 %shard_map.28 = (bf16[3584,1024]{1,0:T(8,128)(2,1)}, bf16[3,3584,3584]{2,1,0:T(8,128)(2,1)}, bf16[4,3584,3584]{2,1,0:T(8,128)(2,1)}, bf16[4,3584,1024]{2,1,0:T(8,128)(2,1)}) custom-call(bf16[3584,3584]{1,0:T(8,128)(2,1)} %tri.1, bf16[3584,1024]{1,0:T(8,128)(2,1)} %rhs.1), custom_call_target="tpu_custom_call" | custom-call | tf_op jit(solution)/shard_map/pallas_call | solution.py:373
  480.5 7.0 %copy.4 = bf16[3584,1024]{1,0:T(8,128)(2,1)} copy(bf16[3584,1024]{1,0:T(8,128)(2,1)} %get-tuple-element.6) | data formatting | bytes 14680064

commit v2 on v1

--- a/solution.py
+++ b/solution.py
@@ -9,9 +9,8 @@
 
 BLOCK_SIZE = 256
 NEAR_STEPS = 6
-LAG = 3
-AHEAD = 4
-SLOTS = 4
+AHEAD = 1
+SLOTS = 5
 MESH = pl.DeviceIdType.MESH
 
 
@@ -30,7 +29,7 @@
 
 
 def kernel(bs, nb, near, tri, rhs, out, l_got, l_end, b_got, acc, part, l_tile, b_tile, o_tile, sems, l_sem, b_sem, o_sem):
-    (ys, yr, ds, dr, fs, fr, b1s, b1r, l0s, l0r, l2s, l2r, e0s, e0r, e2s, e2r,
+    (ys, yr, ds, dr, fs, fr, b1s, b1r, l0s, l0r, l2s, l2r, e0s, e0r, e2s, e2r, l3s, l3r, e3s, e3r,
      os_, or_, ws, wr, ms, mr, us, ur, vs, vr, ps, pr) = sems
     g, z, c = lax.axis_index("batch"), lax.axis_index("row"), lax.axis_index("col")
     is_end = lax.rem(z, 3) == 0
@@ -69,6 +68,12 @@
     def e2_copy(s):
         return send(panel(l_end, s, 2), panel(l_end, s, 3), e2s.at[s - near], e2r.at[s - near], (g, z, sib))
 
+    def l3_copy(s):
+        return send(panel(l_got, s, 2), panel(l_end, s, 3), l3s.at[s - near], l3r.at[s - near], (g, ze, c))
+
+    def e3_copy(s):
+        return send(panel(l_end, s, 3), panel(l_end, s, 2), e3s.at[s - near], e3r.at[s - near], (g, z, sib))
+
     def b_copy(owner, n, ss, rs, dev):
         return send(rhs.at[rows(n)], b_got.at[owner, rows(n)], ss.at[n], rs.at[n], dev)
 
@@ -118,10 +123,8 @@
             @pl.when(owner != z)
             def _():
                 pltpu.make_async_copy(b_got.at[owner, rows(load_b.step)], to, b_sem.at[i]).start()
-        for i, owner in slots:
-            pltpu.make_async_copy(rhs.at[rows(0)], b_tile.at[pl.ds(i * bs, bs)], b_sem.at[i]).wait()
-
-    def tiles(s, start_tile, depth, target, base):
+
+    def tiles(s, start_tile, depth, target, base, after_first=None):
         def start(j):
             start_tile(j, lax.rem(j - s, SLOTS))
 
@@ -134,6 +137,8 @@
             @pl.when(s + d < nb)
             def _():
                 start(s + d)
+        for i in range(depth):
+            pltpu.make_async_copy(rhs.at[rows(0)], b_tile.at[pl.ds(i * bs, bs)], b_sem.at[i]).wait()
 
         @pl.loop(s, nb)
         def _(j):
@@ -143,6 +148,11 @@
 
             slot = lax.rem(j - s, SLOTS)
             wait(slot)
+            if after_first is not None:
+                @pl.when(j == s + 1)
+                def _():
+                    after_first()
+
             at = pl.ds(pl.multiple_of((j - base) * bs, bs), bs)
             target[at, :] += jnp.dot(
                 l_tile[slot, :, : depth * bs], b_tile[: depth * bs, :], preferred_element_type=jnp.float32
@@ -189,20 +199,44 @@
             for t in range(1, 4):
                 l_copy(l_end.at[flip(r0, t)], j, s, slot, t - 1).start()
 
-        tiles(s, start_tile, 3, part, near)
+        tiles(s, start_tile, 3, part, near, lambda: p_copy(s).start())
+
+        @pl.when(s == nb - 1)
+        def _():
+            p_copy(s).start()
 
     def finish(j, extra):
         at = rows(j)
         total = acc[at, :]
         if extra:
             total = total + part[pl.ds(pl.multiple_of((j - near) * bs, bs), bs), :]
-        o_tile[...] = total.astype(o_tile.dtype)
-        copy = pltpu.make_async_copy(o_tile, out.at[at], o_sem)
-        copy.start()
-        copy.wait()
-
+        slot = lax.rem(j, 2)
+
+        @pl.when(j >= 2)
+        def _():
+            o_copy_out(j - 2).wait()
+
+        o_tile[slot] = total.astype(o_tile.dtype)
+        o_copy_out(j).start()
+
+    def o_copy_out(j):
+        slot = lax.rem(j, 2)
+        return pltpu.make_async_copy(o_tile.at[slot], out.at[rows(j)], o_sem.at[slot])
+
+    gives0, gives2 = c != z, across != z
     has0, has2 = c != ze, across != ze
-    gives0, gives2 = c != z, across != z
+    light = lax.rem(c + z, 2) == 0
+    light_there = lax.rem(c + ze, 2) == 0
+    heavy, heavy_there = jnp.logical_not(light), jnp.logical_not(light_there)
+
+    def swapped(s):
+        return (s - near) % 2 == 1
+
+    def over2(s):
+        return jnp.logical_and(gives2, light) if swapped(s) else gives2
+
+    def got2(s):
+        return jnp.logical_and(has2, light_there) if swapped(s) else has2
 
     @pl.when(is_end)
     def _():
@@ -210,24 +244,26 @@
             y_copy(s).start()
         for s in range(nb):
             d_copy(s).start()
-        sent = 0
-        for j in range(near, nb):
-            upto = min(4 + 2 * (j - near), j + 2) if j < nb - 1 else nb - 2
-            for n in range(sent, upto):
-                b1_copy(n).start()
-            sent = max(sent, upto)
-            pass_on(j)
+        order = sorted([(2 * n + 1, n, False) for n in range(nb)] + [(2 * j + 2, j, True) for j in range(near, nb)])
+        for _, i, is_l in order:
+            if not is_l:
+                b1_copy(i).start()
+                continue
+            pass_on(i)
 
             @pl.when(gives0)
             def _():
-                l0_copy(j).start()
-
-            @pl.when(gives2)
-            def _():
-                l2_copy(j).start()
-
-        for n in range(sent, nb):
-            b1_copy(n).start()
+                l0_copy(i).start()
+
+            @pl.when(over2(i))
+            def _():
+                l2_copy(i).start()
+
+            if swapped(i):
+                @pl.when(light)
+                def _():
+                    f_copy(i).wait_recv()
+                    l3_copy(i).start()
 
         acc[...] = jnp.zeros_like(acc)
 
@@ -235,7 +271,12 @@
         def _(s):
             def ready(i):
                 d_copy(i).wait_recv()
-                f_copy(i).wait_recv()
+                if swapped(i):
+                    @pl.when(heavy)
+                    def _():
+                        f_copy(i).wait_recv()
+                else:
+                    f_copy(i).wait_recv()
 
             at_step(s, near, nb, ready)
             diag_step(s)
@@ -258,6 +299,8 @@
             p_copy(j).wait_recv()
             finish(j, True)
 
+        o_copy_out(nb - 2).wait()
+        o_copy_out(nb - 1).wait()
         for s in range(nb):
             y_copy(s).wait_send()
             d_copy(s).wait_send()
@@ -268,9 +311,14 @@
             def _():
                 l0_copy(s).wait_send()
 
-            @pl.when(gives2)
+            @pl.when(over2(s))
             def _():
                 l2_copy(s).wait_send()
+
+            if swapped(s):
+                @pl.when(light)
+                def _():
+                    l3_copy(s).wait_send()
 
     @pl.when(jnp.logical_not(is_end))
     def _():
@@ -285,7 +333,44 @@
         acc[...] = jnp.zeros_like(acc)
         part[...] = jnp.zeros_like(part)
 
-        @pl.loop(0, nb + LAG)
+        def relay(i):
+            @pl.when(has0)
+            def _():
+                l0_copy(i).wait_recv()
+                e0_copy(i).start()
+
+            @pl.when(got2(i))
+            def _():
+                l2_copy(i).wait_recv()
+                e2_copy(i).start()
+
+            if swapped(i):
+                @pl.when(light_there)
+                def _():
+                    l3_copy(i).wait_recv()
+                    e3_copy(i).start()
+
+        def relayed(i):
+            @pl.when(sib != ze)
+            def _():
+                e0_copy(i).wait_recv()
+
+            if swapped(i):
+                @pl.when(heavy_there)
+                def _():
+                    e3_copy(i).wait_recv()
+
+            from_sib = jnp.logical_and(3 - c != ze, heavy_there) if swapped(i) else 3 - c != ze
+
+            @pl.when(from_sib)
+            def _():
+                e2_copy(i).wait_recv()
+
+        def ready(i):
+            d_copy(i).wait_recv()
+            f_copy(i).wait_recv()
+
+        @pl.loop(0, nb + 4)
         def _(n):
             @pl.when(n < nb)
             def _():
@@ -304,44 +389,27 @@
                     u_copy(n).start()
                     v_copy(n).start()
 
-                @pl.when(n >= near)
-                def _():
-                    def relay(i):
-                        @pl.when(has0)
-                        def _():
-                            l0_copy(i).wait_recv()
-                            e0_copy(i).start()
-
-                        @pl.when(has2)
-                        def _():
-                            l2_copy(i).wait_recv()
-                            e2_copy(i).start()
-
-                        @pl.when(sib != ze)
-                        def _():
-                            e0_copy(i).wait_recv()
-
-                        @pl.when(3 - c != ze)
-                        def _():
-                            e2_copy(i).wait_recv()
-
-                    at_step(n, near, nb, relay)
-                    end_step(n)
-                    p_copy(n).start()
-
-            @pl.when(n >= LAG)
-            def _():
-                s = n - LAG
-
-                def ready(i):
-                    pass_on(i)
-                    d_copy(i).wait_recv()
-                    f_copy(i).wait_recv()
-
+                at_step(n, near, nb, relay)
+
+            @pl.when(jnp.logical_and(n > near, n <= nb))
+            def _():
+                at_step(n - 1, near, nb, relayed)
+                end_step(n - 1)
+
+            @pl.when(n == 1)
+            def _():
+                pass_on(0)
+
+            @pl.when(jnp.logical_and(n >= 2, jnp.logical_and(n != 4, n != 6)))
+            def _():
+                s = n - 2 - (n > 3).astype(jnp.int32) - (n > 5).astype(jnp.int32)
                 at_step(s, 0, nb, ready)
                 own_step(s)
                 finish(s, False)
-
+                at_step(s + 1, 1, nb, pass_on)
+
+        o_copy_out(nb - 2).wait()
+        o_copy_out(nb - 1).wait()
         for s in range(nb):
             y_copy(s).wait_send()
             d_copy(s).wait_send()
@@ -359,9 +427,14 @@
             def _():
                 e0_copy(s).wait_send()
 
-            @pl.when(has2)
+            @pl.when(got2(s))
             def _():
                 e2_copy(s).wait_send()
+
+            if swapped(s):
+                @pl.when(light_there)
+                def _():
+                    e3_copy(s).wait_send()
 
 
 def local_trmm(tri, rhs, bs=BLOCK_SIZE, near=NEAR_STEPS):
@@ -369,7 +442,7 @@
     nb = size // bs
     far = nb - near
     any_spec = pl.BlockSpec(memory_space=pl.ANY)
-    counts = [nb] * 8 + [far] * 8 + [nb] * 4 + [near] * 6 + [far] * 2
+    counts = [nb] * 8 + [far] * 12 + [nb] * 4 + [near] * 6 + [far] * 2
     return pl.pallas_call(
         functools.partial(kernel, bs, nb, near),
         out_shape=[
@@ -385,11 +458,11 @@
             pltpu.VMEM((far * bs, cols), jnp.float32),
             pltpu.VMEM((SLOTS, bs, 4 * bs), jnp.bfloat16),
             pltpu.VMEM((4 * bs, cols), jnp.bfloat16),
-            pltpu.VMEM((bs, cols), jnp.bfloat16),
+            pltpu.VMEM((2, bs, cols), jnp.bfloat16),
             tuple(pltpu.SemaphoreType.DMA((n,)) for n in counts),
             pltpu.SemaphoreType.DMA((SLOTS, 4)),
             pltpu.SemaphoreType.DMA((4,)),
-            pltpu.SemaphoreType.DMA,
+            pltpu.SemaphoreType.DMA((2,)),
         ],
         compiler_params=pltpu.CompilerParams(has_side_effects=True, vmem_limit_bytes=56 * 2**20),
     )(tri, rhs)[0]

time: 489 us -> 404 us (0.83)
  Pallas kernels: 480 us -> 396 us
    pallas_call x1, Pallas kernels: 480 us -> 396 us  [local_trmm(): pl.pallas_call(functools.partial(kernel, bs, nb, near), out_shape=[jax.Sh...]
where the time goes in v2:
time: 404 us; the launch traced here: 403 us
  Pallas kernels  396 us (98%)
  local copies, waits for them, and re-layouts  6.98 us (2%)
    pallas_call x1, Pallas kernels, local_trmm(): pl.pallas_call(functools.partial(kernel, bs, nb, near), out_shape=[jax.Sh...  396 us

profile of v2, /device:TPU:0, one launch (start us, length us, event | category | flops | bytes accessed | tf_op | source)
XLA Modules:
  0.0 403.1 jit_solution(1316636608611880312)
XLA Ops:
  0.0 396.1 %shard_map.28 = (bf16[3584,1024]{1,0:T(8,128)(2,1)}, bf16[3,3584,3584]{2,1,0:T(8,128)(2,1)}, bf16[4,3584,3584]{2,1,0:T(8,128)(2,1)}, bf16[4,3584,1024]{2,1,0:T(8,128)(2,1)}) custom-call(bf16[3584,3584]{1,0:T(8,128)(2,1)} %tri.1, bf16[3584,1024]{1,0:T(8,128)(2,1)} %rhs.1), custom_call_target="tpu_custom_call" | custom-call | tf_op jit(solution)/shard_map/pallas_call | solution.py:446
  396.1 7.0 %copy.4 = bf16[3584,1024]{1,0:T(8,128)(2,1)} copy(bf16[3584,1024]{1,0:T(8,128)(2,1)} %get-tuple-element.6) | data formatting | bytes 14680064

commit v3 on v2

--- a/solution.py
+++ b/solution.py
@@ -28,7 +28,7 @@
     return lax.rem(a + b, 2) + 2 * lax.rem(a // 2 + b // 2, 2)
 
 
-def kernel(bs, nb, near, tri, rhs, out, l_got, l_end, b_got, acc, part, l_tile, b_tile, o_tile, sems, l_sem, b_sem, o_sem):
+def kernel(bs, nb, near, tri, rhs, out, l_got, l_end, b_got, acc, part, l_tile, b_tile, sems, l_sem, b_sem):
     (ys, yr, ds, dr, fs, fr, b1s, b1r, l0s, l0r, l2s, l2r, e0s, e0r, e2s, e2r, l3s, l3r, e3s, e3r,
      os_, or_, ws, wr, ms, mr, us, ur, vs, vr, ps, pr) = sems
     g, z, c = lax.axis_index("batch"), lax.axis_index("row"), lax.axis_index("col")
@@ -37,6 +37,19 @@
     zo = flip(z, 3)
     sib, across = flip(c, 1), flip(c, 2)
 
+    barrier = pltpu.get_barrier_semaphore()
+    for peer in ((g, z, sib), (g, z, across), (g, ze, c)):
+        pl.semaphore_signal(barrier, inc=1, device_id=peer, device_id_type=MESH)
+
+    @pl.when(jnp.logical_not(is_end))
+    def _():
+        pl.semaphore_signal(barrier, inc=1, device_id=(g, zo, c), device_id_type=MESH)
+        pl.semaphore_wait(barrier, 4)
+
+    @pl.when(is_end)
+    def _():
+        pl.semaphore_wait(barrier, 3)
+
     def rows(s):
         return pl.ds(pl.multiple_of(s * bs, bs), bs)
 
@@ -210,18 +223,7 @@
         total = acc[at, :]
         if extra:
             total = total + part[pl.ds(pl.multiple_of((j - near) * bs, bs), bs), :]
-        slot = lax.rem(j, 2)
-
-        @pl.when(j >= 2)
-        def _():
-            o_copy_out(j - 2).wait()
-
-        o_tile[slot] = total.astype(o_tile.dtype)
-        o_copy_out(j).start()
-
-    def o_copy_out(j):
-        slot = lax.rem(j, 2)
-        return pltpu.make_async_copy(o_tile.at[slot], out.at[rows(j)], o_sem.at[slot])
+        out[at, :] = total.astype(out.dtype)
 
     gives0, gives2 = c != z, across != z
     has0, has2 = c != ze, across != ze
@@ -244,7 +246,7 @@
             y_copy(s).start()
         for s in range(nb):
             d_copy(s).start()
-        order = sorted([(2 * n + 1, n, False) for n in range(nb)] + [(2 * j + 2, j, True) for j in range(near, nb)])
+        order = sorted([(2 * n - 1, n, False) for n in range(nb)] + [(2 * j + 2, j, True) for j in range(near, nb)])
         for _, i, is_l in order:
             if not is_l:
                 b1_copy(i).start()
@@ -299,8 +301,6 @@
             p_copy(j).wait_recv()
             finish(j, True)
 
-        o_copy_out(nb - 2).wait()
-        o_copy_out(nb - 1).wait()
         for s in range(nb):
             y_copy(s).wait_send()
             d_copy(s).wait_send()
@@ -370,16 +370,22 @@
             d_copy(i).wait_recv()
             f_copy(i).wait_recv()
 
+        b1_copy(0).wait_recv()
+        w_copy(0).start()
+        o_copy(AHEAD).start()
+
         @pl.loop(0, nb + 4)
         def _(n):
             @pl.when(n < nb)
             def _():
-                b1_copy(n).wait_recv()
-                w_copy(n).start()
-
-                @pl.when(n + AHEAD < nb)
-                def _():
-                    o_copy(n + AHEAD).start()
+                @pl.when(n + 1 < nb)
+                def _():
+                    b1_copy(n + 1).wait_recv()
+                    w_copy(n + 1).start()
+
+                @pl.when(n + 1 + AHEAD < nb)
+                def _():
+                    o_copy(n + 1 + AHEAD).start()
 
                 o_copy(n).wait_recv()
                 w_copy(n).wait_recv()
@@ -408,8 +414,6 @@
                 finish(s, False)
                 at_step(s + 1, 1, nb, pass_on)
 
-        o_copy_out(nb - 2).wait()
-        o_copy_out(nb - 1).wait()
         for s in range(nb):
             y_copy(s).wait_send()
             d_copy(s).wait_send()
@@ -446,25 +450,23 @@
     return pl.pallas_call(
         functools.partial(kernel, bs, nb, near),
         out_shape=[
-            jax.ShapeDtypeStruct((size, cols), jnp.bfloat16),
+            pltpu.VMEM((size, cols), jnp.bfloat16),
             jax.ShapeDtypeStruct((3, size, size), jnp.bfloat16),
             jax.ShapeDtypeStruct((4, size, size), jnp.bfloat16),
             jax.ShapeDtypeStruct((4, size, cols), jnp.bfloat16),
         ],
         in_specs=[any_spec] * 2,
-        out_specs=[any_spec] * 4,
+        out_specs=[pl.BlockSpec(memory_space=pltpu.VMEM)] + [any_spec] * 3,
         scratch_shapes=[
             pltpu.VMEM((size, cols), jnp.float32),
             pltpu.VMEM((far * bs, cols), jnp.float32),
             pltpu.VMEM((SLOTS, bs, 4 * bs), jnp.bfloat16),
             pltpu.VMEM((4 * bs, cols), jnp.bfloat16),
-            pltpu.VMEM((2, bs, cols), jnp.bfloat16),
             tuple(pltpu.SemaphoreType.DMA((n,)) for n in counts),
             pltpu.SemaphoreType.DMA((SLOTS, 4)),
             pltpu.SemaphoreType.DMA((4,)),
-            pltpu.SemaphoreType.DMA((2,)),
         ],
-        compiler_params=pltpu.CompilerParams(has_side_effects=True, vmem_limit_bytes=56 * 2**20),
+        compiler_params=pltpu.CompilerParams(has_side_effects=True, collective_id=0, vmem_limit_bytes=48 * 2**20),
     )(tri, rhs)[0]
 
 

time: 404 us -> 393 us (0.973)
  Pallas kernels: 396 us -> 387 us
    pallas_call x1, Pallas kernels: 396 us -> 387 us  [local_trmm(): pl.pallas_call(functools.partial(kernel, bs, nb, near), out_shape=[pltpu....]
where the time goes in v3:
time: 393 us; the launch traced here: 390 us
  Pallas kernels  387 us (98%)
    pallas_call x1, Pallas kernels, local_trmm(): pl.pallas_call(functools.partial(kernel, bs, nb, near), out_shape=[pltpu....  387 us

profile of v3, /device:TPU:0, one launch (start us, length us, event | category | flops | bytes accessed | tf_op | source)
XLA Modules:
  0.0 390.4 jit_solution(276192600049275216)
XLA Ops:
  0.0 387.3 %shard_map.28 = (bf16[3584,1024]{1,0:T(8,128)(2,1)S(1)}, bf16[3,3584,3584]{2,1,0:T(8,128)(2,1)}, bf16[4,3584,3584]{2,1,0:T(8,128)(2,1)}, bf16[4,3584,1024]{2,1,0:T(8,128)(2,1)}) custom-call(bf16[3584,3584]{1,0:T(8,128)(2,1)} %tri.1, bf16[3584,1024]{1,0:T(8,128)(2,1)} %rhs.1), custom_call_target="tpu_custom_call" | custom-call | tf_op jit(solution)/shard_map/pallas_call | solution.py:450
  387.3 3.1 copy.4

commit v4 on v3

--- a/solution.py
+++ b/solution.py
@@ -8,7 +8,9 @@
 from jax.sharding import PartitionSpec as P
 
 BLOCK_SIZE = 256
-NEAR_STEPS = 6
+NEAR_STEPS = 5
+VIA_Y = 3
+EARLY = 3
 AHEAD = 1
 SLOTS = 5
 MESH = pl.DeviceIdType.MESH
@@ -29,7 +31,7 @@
 
 
 def kernel(bs, nb, near, tri, rhs, out, l_got, l_end, b_got, acc, part, l_tile, b_tile, sems, l_sem, b_sem):
-    (ys, yr, ds, dr, fs, fr, b1s, b1r, l0s, l0r, l2s, l2r, e0s, e0r, e2s, e2r, l3s, l3r, e3s, e3r,
+    (ys, yr, ds, dr, fs, fr, b1s, b1r, l0s, l0r, l2s, l2r, e0s, e0r, e2s, e2r, l3s, l3r, e3s, e3r, y2s, y2r,
      os_, or_, ws, wr, ms, mr, us, ur, vs, vr, ps, pr) = sems
     g, z, c = lax.axis_index("batch"), lax.axis_index("row"), lax.axis_index("col")
     is_end = lax.rem(z, 3) == 0
@@ -87,6 +89,9 @@
     def e3_copy(s):
         return send(panel(l_end, s, 3), panel(l_end, s, 2), e3s.at[s - near], e3r.at[s - near], (g, z, sib))
 
+    def y2_copy(s):
+        return send(panel(l_end, s, 0), panel(l_end, s, 2), y2s.at[s - near], y2r.at[s - near], (g, z, across))
+
     def b_copy(owner, n, ss, rs, dev):
         return send(rhs.at[rows(n)], b_got.at[owner, rows(n)], ss.at[n], rs.at[n], dev)
 
@@ -231,8 +236,11 @@
     light_there = lax.rem(c + ze, 2) == 0
     heavy, heavy_there = jnp.logical_not(light), jnp.logical_not(light_there)
 
+    def via_y(s):
+        return s < near + VIA_Y
+
     def swapped(s):
-        return (s - near) % 2 == 1
+        return not via_y(s) and (s - near) % 2 == 1
 
     def over2(s):
         return jnp.logical_and(gives2, light) if swapped(s) else gives2
@@ -246,7 +254,7 @@
             y_copy(s).start()
         for s in range(nb):
             d_copy(s).start()
-        order = sorted([(2 * n - 1, n, False) for n in range(nb)] + [(2 * j + 2, j, True) for j in range(near, nb)])
+        order = sorted([(2 * n - 1, n, False) for n in range(nb)] + [(2 * j + (0 if via_y(j) else 2), j, True) for j in range(near, nb)])
         for _, i, is_l in order:
             if not is_l:
                 b1_copy(i).start()
@@ -256,6 +264,9 @@
             @pl.when(gives0)
             def _():
                 l0_copy(i).start()
+
+            if via_y(i):
+                continue
 
             @pl.when(over2(i))
             def _():
@@ -311,6 +322,9 @@
             def _():
                 l0_copy(s).wait_send()
 
+            if via_y(s):
+                continue
+
             @pl.when(over2(s))
             def _():
                 l2_copy(s).wait_send()
@@ -326,7 +340,7 @@
             o_copy(n).start()
         for n in range(near):
             m_copy(n).start()
-        for s in range(nb):
+        for s in range(EARLY):
             y_copy(s).start()
         for s in range(nb):
             d_copy(s).start()
@@ -337,7 +351,15 @@
             @pl.when(has0)
             def _():
                 l0_copy(i).wait_recv()
+                if via_y(i):
+                    y2_copy(i).start()
                 e0_copy(i).start()
+
+            if i == near + VIA_Y - 1:
+                for s in range(EARLY, nb):
+                    y_copy(s).start()
+            if via_y(i):
+                return
 
             @pl.when(got2(i))
             def _():
@@ -349,6 +371,12 @@
                 def _():
                     l3_copy(i).wait_recv()
                     e3_copy(i).start()
+
+        def crossed(i):
+            @pl.when(has2)
+            def _():
+                y2_copy(i).wait_recv()
+                e2_copy(i).start()
 
         def relayed(i):
             @pl.when(sib != ze)
@@ -374,7 +402,7 @@
         w_copy(0).start()
         o_copy(AHEAD).start()
 
-        @pl.loop(0, nb + 4)
+        @pl.loop(0, nb + 5)
         def _(n):
             @pl.when(n < nb)
             def _():
@@ -395,24 +423,25 @@
                     u_copy(n).start()
                     v_copy(n).start()
 
-                at_step(n, near, nb, relay)
-
-            @pl.when(jnp.logical_and(n > near, n <= nb))
-            def _():
-                at_step(n - 1, near, nb, relayed)
-                end_step(n - 1)
-
-            @pl.when(n == 1)
-            def _():
-                pass_on(0)
-
-            @pl.when(jnp.logical_and(n >= 2, jnp.logical_and(n != 4, n != 6)))
-            def _():
-                s = n - 2 - (n > 3).astype(jnp.int32) - (n > 5).astype(jnp.int32)
+                at_step(n + 1, near, near + VIA_Y, relay)
+                at_step(n, near, near + VIA_Y, crossed)
+                at_step(n, near + VIA_Y, nb, relay)
+
+            @pl.when(jnp.logical_and(n >= near, n < nb))
+            def _():
+                at_step(n, near, nb, relayed)
+                end_step(n)
+
+            @pl.when(jnp.logical_and(n >= 2, jnp.logical_and(n != 4, jnp.logical_or(n < 6, n > 7))))
+            def _():
+                s = n - 2 - (n > 3).astype(jnp.int32) - 2 * (n > 5).astype(jnp.int32)
                 at_step(s, 0, nb, ready)
                 own_step(s)
                 finish(s, False)
-                at_step(s + 1, 1, nb, pass_on)
+
+            at_step(n - 1, 0, 2, pass_on)
+            at_step(n - 2, 2, 3, pass_on)
+            at_step(n - 4, 3, nb, pass_on)
 
         for s in range(nb):
             y_copy(s).wait_send()
@@ -430,8 +459,10 @@
             @pl.when(has0)
             def _():
                 e0_copy(s).wait_send()
-
-            @pl.when(got2(s))
+                if via_y(s):
+                    y2_copy(s).wait_send()
+
+            @pl.when(has2 if via_y(s) else got2(s))
             def _():
                 e2_copy(s).wait_send()
 
@@ -446,7 +477,7 @@
     nb = size // bs
     far = nb - near
     any_spec = pl.BlockSpec(memory_space=pl.ANY)
-    counts = [nb] * 8 + [far] * 12 + [nb] * 4 + [near] * 6 + [far] * 2
+    counts = [nb] * 8 + [far] * 14 + [nb] * 4 + [near] * 6 + [far] * 2
     return pl.pallas_call(
         functools.partial(kernel, bs, nb, near),
         out_shape=[

time: 393 us -> 387 us (0.985)
  Pallas kernels: 387 us -> 379 us
    pallas_call x1, Pallas kernels: 387 us -> 379 us  [local_trmm(): pl.pallas_call(functools.partial(kernel, bs, nb, near), out_shape=[pltpu....]
where the time goes in v4:
time: 387 us; the launch traced here: 382 us
  Pallas kernels  379 us (98%)
    pallas_call x1, Pallas kernels, local_trmm(): pl.pallas_call(functools.partial(kernel, bs, nb, near), out_shape=[pltpu....  379 us

profile of v4, /device:TPU:0, one launch (start us, length us, event | category | flops | bytes accessed | tf_op | source)
XLA Modules:
  0.0 382.4 jit_solution(12245985909684292213)
XLA Ops:
  0.0 379.3 %shard_map.28 = (bf16[3584,1024]{1,0:T(8,128)(2,1)S(1)}, bf16[3,3584,3584]{2,1,0:T(8,128)(2,1)}, bf16[4,3584,3584]{2,1,0:T(8,128)(2,1)}, bf16[4,3584,1024]{2,1,0:T(8,128)(2,1)}) custom-call(bf16[3584,3584]{1,0:T(8,128)(2,1)} %tri.1, bf16[3584,1024]{1,0:T(8,128)(2,1)} %rhs.1), custom_call_target="tpu_custom_call" | custom-call | tf_op jit(solution)/shard_map/pallas_call | solution.py:481
  379.3 3.1 copy.4
